TPU v7x, 32 devices: a whole 2x2x4 slice. The times are simulated.
32 devices in a mesh: ta: 2 (over x), gz: 4 (over z), xy: 4 (over y, core).
Axes of the slice: x: 2, y: 2, z: 4, core: 2. Of those that a mesh axis runs over, the one named last changes fastest.
Arguments:
- source: float32 [2, 48, 2, 4, 512], P(None, None, 'ta', 'gz', 'xy'), may hold values from -14 to 14
- inverse: bfloat16 [2, 48, 48, 2, 4, 512], P(None, None, None, 'ta', 'gz', 'xy'), may hold values from -0.625 to 0.625
- coarse_links: bfloat16 [8, 2, 48, 48, 2, 4, 512], P(None, None, None, None, 'ta', 'gz', 'xy'), may hold values from -0.15625 to 0.15625
Outputs:
- solution: float32 [2, 48, 2, 4, 512], P(None, None, 'ta', 'gz', 'xy')
- residual: float32 [2, 48, 2, 4, 512], P(None, None, 'ta', 'gz', 'xy')
- hessenberg: float32 [2, 6, 5], replicated
All inputs are finite; a program needn't handle non-finite values.
Results may differ from a plain program's by a relative error of at most 0.0003.
Values sent between devices are 32-bit elements; how exact they have to be, the bound alone decides.
A program may use at most 128 MiB of HBM per device.

v0:
```python
import jax
import jax.numpy as jnp
from jax import lax
from jax.sharding import PartitionSpec as P

LY = 16
ITERS = 5


def padded_2(cells, sides, width):
    for axis, dim in sides:
        count = lax.axis_size(axis)
        head = lax.slice_in_dim(cells, 0, width, axis=dim)
        tail = lax.slice_in_dim(cells, cells.shape[dim] - width, cells.shape[dim], axis=dim)
        cells = jnp.concatenate(
            [
                lax.ppermute(tail, axis, [(i, (i + 1) % count) for i in range(count)]),
                cells,
                lax.ppermute(head, axis, [((i + 1) % count, i) for i in range(count)]),
            ],
            axis=dim,
        )
    return cells


def block_apply(blocks, vector):
    real_blocks = blocks[0].astype(jnp.float32)
    imag_blocks = blocks[1].astype(jnp.float32)
    vec_real = vector[0][None]
    vec_imag = vector[1][None]
    real_part = jnp.sum(real_blocks * vec_real - imag_blocks * vec_imag, axis=1)
    imag_part = jnp.sum(real_blocks * vec_imag + imag_blocks * vec_real, axis=1)
    return jnp.stack([real_part, imag_part])


def complex_dot(left, right):
    real_part = jnp.sum(left[0] * right[0] + left[1] * right[1])
    imag_part = jnp.sum(left[0] * right[1] - left[1] * right[0])
    return (real_part, imag_part)


def scaled(coef_real, coef_imag, vector):
    return jnp.stack(
        [
            coef_real * vector[0] - coef_imag * vector[1],
            coef_real * vector[1] + coef_imag * vector[0],
        ]
    )


def y_neighbours(field):
    positions = jnp.arange(field.shape[4]) % LY
    is_last = positions == LY - 1
    is_first = positions == 0
    forward = jnp.where(is_last, jnp.roll(field, LY - 1, axis=4), jnp.roll(field, -1, axis=4))
    backward = jnp.where(is_first, jnp.roll(field, 1 - LY, axis=4), jnp.roll(field, 1, axis=4))
    return (forward, backward)


def apply_operator(field, inverse, coarse_links):
    padded = padded_2(field, (("ta", 2), ("gz", 3)), 1)
    widened = padded_2(field, (("xy", 4),), LY)
    extent = field.shape[4]
    forward_y, backward_y = y_neighbours(field)
    neighbours = [
        padded[:, :, 2:, 1:-1],
        padded[:, :, :-2, 1:-1],
        padded[:, :, 1:-1, 2:],
        padded[:, :, 1:-1, :-2],
        widened[..., 2 * LY : 2 * LY + extent],
        widened[..., :extent],
        forward_y,
        backward_y,
    ]
    hopping = block_apply(coarse_links[0], neighbours[0])
    for d in range(1, 8):
        hopping = hopping + block_apply(coarse_links[d], neighbours[d])
    return field + block_apply(inverse, hopping)


def solve_small(hessenberg, source_norm):
    upper_half = jnp.concatenate([hessenberg[0], -hessenberg[1]], axis=1)
    lower_half = jnp.concatenate([hessenberg[1], hessenberg[0]], axis=1)
    real_form = jnp.concatenate([upper_half, lower_half], axis=0)
    target = jnp.zeros((2 * (ITERS + 1),), jnp.float32).at[0].set(source_norm)
    normal_mat = jnp.dot(real_form.T, real_form, precision=lax.Precision.HIGHEST)
    projected = jnp.dot(real_form.T, target, precision=lax.Precision.HIGHEST)
    factor = jnp.linalg.cholesky(normal_mat)
    forward_vals = []
    for i in range(2 * ITERS):
        partial_sum = projected[i]
        for k in range(i):
            partial_sum = partial_sum - factor[i, k] * forward_vals[k]
        forward_vals.append(partial_sum / factor[i, i])
    solved = [None] * (2 * ITERS)
    for i in reversed(range(2 * ITERS)):
        partial_sum = forward_vals[i]
        for k in range(i + 1, 2 * ITERS):
            partial_sum = partial_sum - factor[k, i] * solved[k]
        solved[i] = partial_sum / factor[i, i]
    coeffs = jnp.stack(solved)
    return (coeffs[:ITERS], coeffs[ITERS:], target)


def per_device(source, inverse, coarse_links):
    norm_sq = lax.psum(complex_dot(source, source)[0], ("ta", "gz", "xy"))
    source_norm = jnp.sqrt(norm_sq)
    krylov_basis = [source / source_norm]
    hessenberg = jnp.zeros((2, ITERS + 1, ITERS), jnp.float32)
    for j in range(ITERS):
        candidate = apply_operator(krylov_basis[j], inverse, coarse_links)
        local_pairs = [complex_dot(krylov_basis[i], candidate) for i in range(j + 1)]
        whole_local = complex_dot(candidate, candidate)[0]
        proj_reals, proj_imags, whole_sq = lax.psum(
            (
                jnp.stack([entry[0] for entry in local_pairs]),
                jnp.stack([entry[1] for entry in local_pairs]),
                whole_local,
            ),
            ("ta", "gz", "xy"),
        )
        for i in range(j + 1):
            candidate = candidate - scaled(proj_reals[i], proj_imags[i], krylov_basis[i])
            hessenberg = hessenberg.at[0, i, j].set(proj_reals[i]).at[1, i, j].set(proj_imags[i])
        length_sq = whole_sq - jnp.sum(proj_reals * proj_reals + proj_imags * proj_imags)
        length = jnp.sqrt(length_sq)
        hessenberg = hessenberg.at[0, j + 1, j].set(length)
        krylov_basis.append(candidate / length)
    coef_real, coef_imag, target = solve_small(hessenberg, source_norm)
    solution = scaled(coef_real[0], coef_imag[0], krylov_basis[0])
    for j in range(1, ITERS):
        solution = solution + scaled(coef_real[j], coef_imag[j], krylov_basis[j])
    residual = source - apply_operator(solution, inverse, coarse_links)
    return (solution, residual, hessenberg)


def solution(mesh):
    return jax.shard_map(
        per_device,
        mesh=mesh,
        in_specs=(
            P(None, None, "ta", "gz", "xy"),
            P(None, None, None, "ta", "gz", "xy"),
            P(None, None, None, None, "ta", "gz", "xy"),
        ),
        out_specs=(P(None, None, "ta", "gz", "xy"), P(None, None, "ta", "gz", "xy"), P()),
        check_vma=False,
    )
```

profile of v0, /device:TPU:0, one launch (start us, length us, event | category | flops | bytes accessed | tf_op | source)
XLA Modules:
  0.0 561.9 jit_solution(17427624493626627391)
XLA Ops:
  2.1 42.2 %psum.112 = f32[]{:T(128)} all-reduce(f32[]{:T(128)} %add_reduce_fusion.20), channel_id=1, replica_groups=mesh['ta'=2,'gz'=4,'xy'=4] {'ta','gz','xy'}, use_global_device_ids=true, to_apply=%region_1.0 | all-reduce | flops 1 | bytes 8 | tf_op jit(solution)/shard_map/psum | solution.py:106
  53.1 3.7 fusion.169
  59.2 3.0 fusion.25
  63.5 4.9 collective-permute-done.3
  68.4 3.8 fusion.97
  73.8 38.8 %all-reduce.6 = (f32[1]{0:T(128)}, f32[1]{0:T(128)}, f32[]{:T(128)}) all-reduce(f32[1]{0:T(128)} %bitcast.81, f32[1]{0:T(128)} %bitcast.83, f32[]{:T(128)} %get-tuple-element.653), channel_id=1, replica_groups=mesh['ta'=2,'gz'=4,'xy'=4] {'ta','gz','xy'}, use_global_device_ids=true, to_apply=%region_21.22 | all-reduce | flops 3 | bytes 24 | tf_op jit(solution)/shard_map/psum | solution.py:114
  125.7 3.7 fusion.173
  133.4 3.0 fusion.29
  139.9 3.7 fusion.101
  148.0 38.8 %all-reduce.5 = (f32[2]{0:T(128)S(1)}, f32[2]{0:T(128)S(1)}, f32[]{:T(128)}) all-reduce(f32[2]{0:T(128)S(1)} %pad_maximum_fusion.30, f32[2]{0:T(128)S(1)} %pad_maximum_fusion.31, f32[]{:T(128)} %get-tuple-element.650), channel_id=1, replica_groups=mesh['ta'=2,'gz'=4,'xy'=4] {'ta','gz','xy'}, use_global_device_ids=true, to_apply=%region_46.47 | all-reduce | flops 5 | bytes 40 | tf_op jit(solution)/shard_map/psum | solution.py:114
  201.3 3.7 fusion.177
  207.2 3.0 fusion.33
  211.1 4.2 collective-permute-done.15
  215.3 3.7 fusion.105
  224.6 39.9 %all-reduce.4 = (f32[3]{0:T(128)S(1)}, f32[3]{0:T(128)S(1)}, f32[]{:T(128)}) all-reduce(f32[3]{0:T(128)S(1)} %pad_maximum_fusion.32, f32[3]{0:T(128)S(1)} %pad_maximum_fusion.33, f32[]{:T(128)} %get-tuple-element.647), channel_id=1, replica_groups=mesh['ta'=2,'gz'=4,'xy'=4] {'ta','gz','xy'}, use_global_device_ids=true, to_apply=%region_74.75 | all-reduce | flops 7 | bytes 56 | tf_op jit(solution)/shard_map/psum | solution.py:114
  277.9 2.7 scatter.136
  283.6 3.7 fusion.181
  289.5 3.0 fusion.37
  293.4 4.6 collective-permute-done.21
  298.1 3.7 fusion.109
  308.8 39.9 %all-reduce.3 = (f32[4]{0:T(128)S(1)}, f32[4]{0:T(128)S(1)}, f32[]{:T(128)}) all-reduce(f32[4]{0:T(128)S(1)} %pad_maximum_fusion.34, f32[4]{0:T(128)S(1)} %pad_maximum_fusion.35, f32[]{:T(128)} %get-tuple-element.642), channel_id=1, replica_groups=mesh['ta'=2,'gz'=4,'xy'=4] {'ta','gz','xy'}, use_global_device_ids=true, to_apply=%region_104.105 | all-reduce | flops 9 | bytes 72 | tf_op jit(solution)/shard_map/psum | solution.py:114
  368.9 3.7 fusion.185
  374.9 3.0 fusion.41
  378.7 4.4 collective-permute-done.27
  383.2 3.7 fusion.113
  389.1 3.2 stack.868
  392.3 3.3 stack.862
  395.6 40.1 %all-reduce.2 = (f32[5]{0:T(128)S(1)}, f32[5]{0:T(128)S(1)}, f32[]{:T(128)}) all-reduce(f32[5]{0:T(128)S(1)} %stack.862, f32[5]{0:T(128)S(1)} %stack.868, f32[]{:T(128)} %get-tuple-element.751), channel_id=1, replica_groups=mesh['ta'=2,'gz'=4,'xy'=4] {'ta','gz','xy'}, use_global_device_ids=true, to_apply=%region_136.137 | all-reduce | flops 11 | bytes 88 | tf_op jit(solution)/shard_map/psum | solution.py:114
  542.8 3.7 fusion.189
  548.8 3.0 fusion.45
  552.8 3.5 collective-permute-done.33
  556.3 3.7 fusion.117
  (290 shorter events, 140.4 us)
Async XLA Ops:
  45.8 11.1 %collective-permute-start = (f32[2,48,1,1,128]{4,3,2,1,0:T(1,128)S(1)}, f32[2,48,1,1,128]{4,3,2,1,0:T(1,128)S(1)}, u32[]{:S(2)}, u32[]{:S(2)}) collective-permute-start(f32[2,48,1,1,128]{4,3,2,1,0:T(1,128)S(1)} %broadcast_divide_fusion), channel_id=1, source_target_pairs={{16,0},{0,16},{17,1},{1,17},{18,2},{2,18},{19,3},{3,19},{20,4},{4,... | collective-permute-start | bytes 147464 | tf_op jit(solution)/shard_map/ppermute | solution.py:19
  48.1 8.7 %collective-permute-start.1 = (f32[2,48,1,1,128]{4,3,2,1,0:T(1,128)S(1)}, f32[2,48,1,1,128]{4,3,2,1,0:T(1,128)S(1)}, u32[]{:S(2)}, u32[]{:S(2)}) collective-permute-start(f32[2,48,1,1,128]{4,3,2,1,0:T(1,128)S(1)} %broadcast_divide_fusion), channel_id=1, source_target_pairs={{0,16},{16,0},{1,17},{17,1},{2,18},{18,2},{3,19},{19,3},{4,20},{20... | collective-permute-start | bytes 147464 | tf_op jit(solution)/shard_map/ppermute | solution.py:17
  48.4 4.4 collective-permute-start.5
  57.0 6.5 %collective-permute-start.2 = (f32[2,48,3,1,128]{4,3,2,1,0:T(1,128)S(1)}, f32[2,48,3,1,128]{4,3,2,1,0:T(1,128)S(1)}, u32[]{:S(2)}, u32[]{:S(2)}) collective-permute-start(f32[2,48,3,1,128]{4,3,2,1,0:T(1,128)S(1)} %pad_maximum_fusion), channel_id=1, source_target_pairs={{4,0},{8,4},{12,8},{0,12},{5,1},{9,5},{13,9},{1,13},{6,2},{10,6},{... | collective-permute-start | bytes 442376 | tf_op jit(solution)/shard_map/ppermute | solution.py:19
  59.2 9.1 %collective-permute-start.3 = (f32[2,48,3,1,128]{4,3,2,1,0:T(1,128)S(1)}, f32[2,48,3,1,128]{4,3,2,1,0:T(1,128)S(1)}, u32[]{:S(2)}, u32[]{:S(2)}) collective-permute-start(f32[2,48,3,1,128]{4,3,2,1,0:T(1,128)S(1)} %pad_maximum_fusion), channel_id=1, source_target_pairs={{0,4},{4,8},{8,12},{12,0},{1,5},{5,9},{9,13},{13,1},{2,6},{6,10},{... | collective-permute-start | bytes 442376 | tf_op jit(solution)/shard_map/ppermute | solution.py:17
  118.2 11.2 %collective-permute-start.6 = (f32[2,48,1,1,128]{4,3,2,1,0:T(1,128)S(1)}, f32[2,48,1,1,128]{4,3,2,1,0:T(1,128)S(1)}, u32[]{:S(2)}, u32[]{:S(2)}) collective-permute-start(f32[2,48,1,1,128]{4,3,2,1,0:T(1,128)S(1)} %fusion.222), channel_id=1, source_target_pairs={{16,0},{0,16},{17,1},{1,17},{18,2},{2,18},{19,3},{3,19},{20,4},{4,... | collective-permute-start | bytes 147464 | tf_op jit(solution)/shard_map/ppermute | solution.py:19
  120.5 8.9 %collective-permute-start.7 = (f32[2,48,1,1,128]{4,3,2,1,0:T(1,128)S(1)}, f32[2,48,1,1,128]{4,3,2,1,0:T(1,128)S(1)}, u32[]{:S(2)}, u32[]{:S(2)}) collective-permute-start(f32[2,48,1,1,128]{4,3,2,1,0:T(1,128)S(1)} %fusion.222), channel_id=1, source_target_pairs={{0,16},{16,0},{1,17},{17,1},{2,18},{18,2},{3,19},{19,3},{4,20},{20... | collective-permute-start | bytes 147464 | tf_op jit(solution)/shard_map/ppermute | solution.py:17
  121.0 4.4 collective-permute-start.11
  129.6 8.6 %collective-permute-start.9 = (f32[2,48,3,1,128]{4,3,2,1,0:T(1,128)S(1)}, f32[2,48,3,1,128]{4,3,2,1,0:T(1,128)S(1)}, u32[]{:S(2)}, u32[]{:S(2)}) collective-permute-start(f32[2,48,3,1,128]{4,3,2,1,0:T(1,128)S(1)} %pad_maximum_fusion.1), channel_id=1, source_target_pairs={{0,4},{4,8},{8,12},{12,0},{1,5},{5,9},{9,13},{13,1},{2,6},{6,10},{... | collective-permute-start | bytes 442376 | tf_op jit(solution)/shard_map/ppermute | solution.py:17
  131.1 8.8 %collective-permute-start.8 = (f32[2,48,3,1,128]{4,3,2,1,0:T(1,128)S(1)}, f32[2,48,3,1,128]{4,3,2,1,0:T(1,128)S(1)}, u32[]{:S(2)}, u32[]{:S(2)}) collective-permute-start(f32[2,48,3,1,128]{4,3,2,1,0:T(1,128)S(1)} %pad_maximum_fusion.1), channel_id=1, source_target_pairs={{4,0},{8,4},{12,8},{0,12},{5,1},{9,5},{13,9},{1,13},{6,2},{10,6},{... | collective-permute-start | bytes 442376 | tf_op jit(solution)/shard_map/ppermute | solution.py:19
  193.7 11.3 %collective-permute-start.12 = (f32[2,48,1,1,128]{4,3,2,1,0:T(1,128)S(1)}, f32[2,48,1,1,128]{4,3,2,1,0:T(1,128)S(1)}, u32[]{:S(2)}, u32[]{:S(2)}) collective-permute-start(f32[2,48,1,1,128]{4,3,2,1,0:T(1,128)S(1)} %fusion.262), channel_id=1, source_target_pairs={{16,0},{0,16},{17,1},{1,17},{18,2},{2,18},{19,3},{3,19},{20,4},{4,... | collective-permute-start | bytes 147464 | tf_op jit(solution)/shard_map/ppermute | solution.py:19
  196.0 9.0 %collective-permute-start.13 = (f32[2,48,1,1,128]{4,3,2,1,0:T(1,128)S(1)}, f32[2,48,1,1,128]{4,3,2,1,0:T(1,128)S(1)}, u32[]{:S(2)}, u32[]{:S(2)}) collective-permute-start(f32[2,48,1,1,128]{4,3,2,1,0:T(1,128)S(1)} %fusion.262), channel_id=1, source_target_pairs={{0,16},{16,0},{1,17},{17,1},{2,18},{18,2},{3,19},{19,3},{4,20},{20... | collective-permute-start | bytes 147464 | tf_op jit(solution)/shard_map/ppermute | solution.py:17
  196.4 4.5 collective-permute-start.16
  196.5 4.4 collective-permute-start.17
  205.1 5.9 %collective-permute-start.14 = (f32[2,48,3,1,128]{4,3,2,1,0:T(1,128)S(1)}, f32[2,48,3,1,128]{4,3,2,1,0:T(1,128)S(1)}, u32[]{:S(2)}, u32[]{:S(2)}) collective-permute-start(f32[2,48,3,1,128]{4,3,2,1,0:T(1,128)S(1)} %pad_maximum_fusion.2), channel_id=1, source_target_pairs={{4,0},{8,4},{12,8},{0,12},{5,1},{9,5},{13,9},{1,13},{6,2},{10,6},{... | collective-permute-start | bytes 442376 | tf_op jit(solution)/shard_map/ppermute | solution.py:19
  206.8 8.5 %collective-permute-start.15 = (f32[2,48,3,1,128]{4,3,2,1,0:T(1,128)S(1)}, f32[2,48,3,1,128]{4,3,2,1,0:T(1,128)S(1)}, u32[]{:S(2)}, u32[]{:S(2)}) collective-permute-start(f32[2,48,3,1,128]{4,3,2,1,0:T(1,128)S(1)} %pad_maximum_fusion.2), channel_id=1, source_target_pairs={{0,4},{4,8},{8,12},{12,0},{1,5},{5,9},{9,13},{13,1},{2,6},{6,10},{... | collective-permute-start | bytes 442376 | tf_op jit(solution)/shard_map/ppermute | solution.py:17
  272.8 14.4 %collective-permute-start.18 = (f32[2,48,1,1,128]{4,3,2,1,0:T(1,128)S(1)}, f32[2,48,1,1,128]{4,3,2,1,0:T(1,128)S(1)}, u32[]{:S(2)}, u32[]{:S(2)}) collective-permute-start(f32[2,48,1,1,128]{4,3,2,1,0:T(1,128)S(1)} %fusion.263), channel_id=1, source_target_pairs={{16,0},{0,16},{17,1},{1,17},{18,2},{2,18},{19,3},{3,19},{20,4},{4,... | collective-permute-start | bytes 147464 | tf_op jit(solution)/shard_map/ppermute | solution.py:19
  275.2 12.1 %collective-permute-start.19 = (f32[2,48,1,1,128]{4,3,2,1,0:T(1,128)S(1)}, f32[2,48,1,1,128]{4,3,2,1,0:T(1,128)S(1)}, u32[]{:S(2)}, u32[]{:S(2)}) collective-permute-start(f32[2,48,1,1,128]{4,3,2,1,0:T(1,128)S(1)} %fusion.263), channel_id=1, source_target_pairs={{0,16},{16,0},{1,17},{17,1},{2,18},{18,2},{3,19},{19,3},{4,20},{20... | collective-permute-start | bytes 147464 | tf_op jit(solution)/shard_map/ppermute | solution.py:17
  275.5 7.7 %collective-permute-start.22 = (f32[2,48,1,1,16]{4,3,2,1,0:T(1,128)S(1)}, f32[2,48,1,1,16]{4,3,2,1,0:T(1,128)S(1)}, u32[]{:S(2)}, u32[]{:S(2)}) collective-permute-start(f32[2,48,1,1,16]{4,3,2,1,0:T(1,128)S(1)} %get-tuple-element.797), channel_id=1, source_target_pairs={{1,0},{2,1},{3,2},{0,3},{5,4},{6,5},{7,6},{4,7},{9,8},{10,9},{11,1... | collective-permute-start | bytes 18440 | tf_op jit(solution)/shard_map/ppermute | solution.py:19
  275.6 7.6 %collective-permute-start.23 = (f32[2,48,1,1,16]{4,3,2,1,0:T(1,128)S(1)}, f32[2,48,1,1,16]{4,3,2,1,0:T(1,128)S(1)}, u32[]{:S(2)}, u32[]{:S(2)}) collective-permute-start(f32[2,48,1,1,16]{4,3,2,1,0:T(1,128)S(1)} %get-tuple-element.796), channel_id=1, source_target_pairs={{0,1},{1,2},{2,3},{3,0},{4,5},{5,6},{6,7},{7,4},{8,9},{9,10},{10,1... | collective-permute-start | bytes 18440 | tf_op jit(solution)/shard_map/ppermute | solution.py:17
  287.4 5.9 %collective-permute-start.20 = (f32[2,48,3,1,128]{4,3,2,1,0:T(1,128)S(1)}, f32[2,48,3,1,128]{4,3,2,1,0:T(1,128)S(1)}, u32[]{:S(2)}, u32[]{:S(2)}) collective-permute-start(f32[2,48,3,1,128]{4,3,2,1,0:T(1,128)S(1)} %pad_maximum_fusion.3), channel_id=1, source_target_pairs={{4,0},{8,4},{12,8},{0,12},{5,1},{9,5},{13,9},{1,13},{6,2},{10,6},{... | collective-permute-start | bytes 442376 | tf_op jit(solution)/shard_map/ppermute | solution.py:19
  289.5 8.5 %collective-permute-start.21 = (f32[2,48,3,1,128]{4,3,2,1,0:T(1,128)S(1)}, f32[2,48,3,1,128]{4,3,2,1,0:T(1,128)S(1)}, u32[]{:S(2)}, u32[]{:S(2)}) collective-permute-start(f32[2,48,3,1,128]{4,3,2,1,0:T(1,128)S(1)} %pad_maximum_fusion.3), channel_id=1, source_target_pairs={{0,4},{4,8},{8,12},{12,0},{1,5},{5,9},{9,13},{13,1},{2,6},{6,10},{... | collective-permute-start | bytes 442376 | tf_op jit(solution)/shard_map/ppermute | solution.py:17
  358.5 14.2 %collective-permute-start.24 = (f32[2,48,1,1,128]{4,3,2,1,0:T(1,128)S(1)}, f32[2,48,1,1,128]{4,3,2,1,0:T(1,128)S(1)}, u32[]{:S(2)}, u32[]{:S(2)}) collective-permute-start(f32[2,48,1,1,128]{4,3,2,1,0:T(1,128)S(1)} %fusion.246), channel_id=1, source_target_pairs={{16,0},{0,16},{17,1},{1,17},{18,2},{2,18},{19,3},{3,19},{20,4},{4,... | collective-permute-start | bytes 147464 | tf_op jit(solution)/shard_map/ppermute | solution.py:19
  360.8 11.8 %collective-permute-start.25 = (f32[2,48,1,1,128]{4,3,2,1,0:T(1,128)S(1)}, f32[2,48,1,1,128]{4,3,2,1,0:T(1,128)S(1)}, u32[]{:S(2)}, u32[]{:S(2)}) collective-permute-start(f32[2,48,1,1,128]{4,3,2,1,0:T(1,128)S(1)} %fusion.246), channel_id=1, source_target_pairs={{0,16},{16,0},{1,17},{17,1},{2,18},{18,2},{3,19},{19,3},{4,20},{20... | collective-permute-start | bytes 147464 | tf_op jit(solution)/shard_map/ppermute | solution.py:17
  361.2 7.4 %collective-permute-start.28 = (f32[2,48,1,1,16]{4,3,2,1,0:T(1,128)S(1)}, f32[2,48,1,1,16]{4,3,2,1,0:T(1,128)S(1)}, u32[]{:S(2)}, u32[]{:S(2)}) collective-permute-start(f32[2,48,1,1,16]{4,3,2,1,0:T(1,128)S(1)} %get-tuple-element.763), channel_id=1, source_target_pairs={{1,0},{2,1},{3,2},{0,3},{5,4},{6,5},{7,6},{4,7},{9,8},{10,9},{11,1... | collective-permute-start | bytes 18440 | tf_op jit(solution)/shard_map/ppermute | solution.py:19
  361.2 7.3 %collective-permute-start.29 = (f32[2,48,1,1,16]{4,3,2,1,0:T(1,128)S(1)}, f32[2,48,1,1,16]{4,3,2,1,0:T(1,128)S(1)}, u32[]{:S(2)}, u32[]{:S(2)}) collective-permute-start(f32[2,48,1,1,16]{4,3,2,1,0:T(1,128)S(1)} %get-tuple-element.762), channel_id=1, source_target_pairs={{0,1},{1,2},{2,3},{3,0},{4,5},{5,6},{6,7},{7,4},{8,9},{9,10},{10,1... | collective-permute-start | bytes 18440 | tf_op jit(solution)/shard_map/ppermute | solution.py:17
  372.8 5.9 %collective-permute-start.26 = (f32[2,48,3,1,128]{4,3,2,1,0:T(1,128)S(1)}, f32[2,48,3,1,128]{4,3,2,1,0:T(1,128)S(1)}, u32[]{:S(2)}, u32[]{:S(2)}) collective-permute-start(f32[2,48,3,1,128]{4,3,2,1,0:T(1,128)S(1)} %pad_maximum_fusion.4), channel_id=1, source_target_pairs={{4,0},{8,4},{12,8},{0,12},{5,1},{9,5},{13,9},{1,13},{6,2},{10,6},{... | collective-permute-start | bytes 442376 | tf_op jit(solution)/shard_map/ppermute | solution.py:19
  374.9 8.3 %collective-permute-start.27 = (f32[2,48,3,1,128]{4,3,2,1,0:T(1,128)S(1)}, f32[2,48,3,1,128]{4,3,2,1,0:T(1,128)S(1)}, u32[]{:S(2)}, u32[]{:S(2)}) collective-permute-start(f32[2,48,3,1,128]{4,3,2,1,0:T(1,128)S(1)} %pad_maximum_fusion.4), channel_id=1, source_target_pairs={{0,4},{4,8},{8,12},{12,0},{1,5},{5,9},{9,13},{13,1},{2,6},{6,10},{... | collective-permute-start | bytes 442376 | tf_op jit(solution)/shard_map/ppermute | solution.py:17
  535.3 11.2 %collective-permute-start.30 = (f32[2,48,1,1,128]{4,3,2,1,0:T(1,128)S(1)}, f32[2,48,1,1,128]{4,3,2,1,0:T(1,128)S(1)}, u32[]{:S(2)}, u32[]{:S(2)}) collective-permute-start(f32[2,48,1,1,128]{4,3,2,1,0:T(1,128)S(1)} %maximum_add_fusion.11), channel_id=1, source_target_pairs={{16,0},{0,16},{17,1},{1,17},{18,2},{2,18},{19,3},{3,19},{20,4},{4,... | collective-permute-start | bytes 147464 | tf_op jit(solution)/shard_map/ppermute | solution.py:19
  537.7 8.8 %collective-permute-start.31 = (f32[2,48,1,1,128]{4,3,2,1,0:T(1,128)S(1)}, f32[2,48,1,1,128]{4,3,2,1,0:T(1,128)S(1)}, u32[]{:S(2)}, u32[]{:S(2)}) collective-permute-start(f32[2,48,1,1,128]{4,3,2,1,0:T(1,128)S(1)} %maximum_add_fusion.11), channel_id=1, source_target_pairs={{0,16},{16,0},{1,17},{17,1},{2,18},{18,2},{3,19},{19,3},{4,20},{20... | collective-permute-start | bytes 147464 | tf_op jit(solution)/shard_map/ppermute | solution.py:17
  546.7 6.0 %collective-permute-start.32 = (f32[2,48,3,1,128]{4,3,2,1,0:T(1,128)S(1)}, f32[2,48,3,1,128]{4,3,2,1,0:T(1,128)S(1)}, u32[]{:S(2)}, u32[]{:S(2)}) collective-permute-start(f32[2,48,3,1,128]{4,3,2,1,0:T(1,128)S(1)} %pad_maximum_fusion.5), channel_id=1, source_target_pairs={{4,0},{8,4},{12,8},{0,12},{5,1},{9,5},{13,9},{1,13},{6,2},{10,6},{... | collective-permute-start | bytes 442376 | tf_op jit(solution)/shard_map/ppermute | solution.py:19
  548.4 7.9 %collective-permute-start.33 = (f32[2,48,3,1,128]{4,3,2,1,0:T(1,128)S(1)}, f32[2,48,3,1,128]{4,3,2,1,0:T(1,128)S(1)}, u32[]{:S(2)}, u32[]{:S(2)}) collective-permute-start(f32[2,48,3,1,128]{4,3,2,1,0:T(1,128)S(1)} %pad_maximum_fusion.5), channel_id=1, source_target_pairs={{0,4},{4,8},{8,12},{12,0},{1,5},{5,9},{9,13},{13,1},{2,6},{6,10},{... | collective-permute-start | bytes 442376 | tf_op jit(solution)/shard_map/ppermute | solution.py:17
  (8 other events, 80.2 us)
where the time goes:
time: 573 us; the launch traced here: 562 us
  blocking collectives  240 us (42%)
  other arithmetic  112 us (20%)
  between operations  88.9 us (16%)
  local copies, waits for them, and re-layouts  52.9 us (9%)
  waiting for transfers between devices  35.3 us (6%)
  starting transfers between devices  32.3 us (6%)
    psum x5, blocking collectives, per_device(): lax.psum((jnp.stack([entry[0] for entry in local_pairs]), jnp.stack([entr...  198 us
    reduce_sum x24, other arithmetic, block_apply(): real_part = jnp.sum(real_blocks * vec_real - imag_blocks * vec_imag, axis=1)  65.3 us
    psum x1, blocking collectives, per_device(): norm_sq = lax.psum(complex_dot(source, source)[0], ('ta', 'gz', 'xy'))  42.2 us
    ppermute x18, waiting for transfers between devices, padded_2(): lax.ppermute(tail, axis, [(i, (i + 1) % count) for i in range(count)])  28.5 us
    ppermute x18, starting transfers between devices, padded_2(): lax.ppermute(head, axis, [((i + 1) % count, i) for i in range(count)])  26.5 us
    scatter x30, local copies, waits for them, and re-layouts, per_device(): hessenberg.at[0, i, j].set(proj_reals[i]).at[1, i, j].set(proj_imags[i])  25.8 us
    sub x15, other arithmetic, scaled(): coef_real * vector[0] - coef_imag * vector[1]  13.2 us
  transfers between devices with their start and end apart: 36, of which 16 were waited for; matrix products, arithmetic and copies ran while one was open for 12% of the time, Pallas kernels for 0%

commit v1 on v0

--- a/solution.py
+++ b/solution.py
@@ -112,12 +112,15 @@
         local_pairs = [complex_dot(krylov_basis[i], candidate) for i in range(j + 1)]
         whole_local = complex_dot(candidate, candidate)[0]
         proj_reals, proj_imags, whole_sq = lax.psum(
-            (
-                jnp.stack([entry[0] for entry in local_pairs]),
-                jnp.stack([entry[1] for entry in local_pairs]),
-                whole_local,
+            lax.psum(
+                (
+                    jnp.stack([entry[0] for entry in local_pairs]),
+                    jnp.stack([entry[1] for entry in local_pairs]),
+                    whole_local,
+                ),
+                ("gz", "xy"),
             ),
-            ("ta", "gz", "xy"),
+            "ta",
         )
         for i in range(j + 1):
             candidate = candidate - scaled(proj_reals[i], proj_imags[i], krylov_basis[i])

time: 573 us -> 544 us (0.949)
  blocking collectives: 240 us -> 223 us
  waiting for transfers between devices: 35.3 us -> 25.3 us
    psum x5, blocking collectives: 198 us -> 153 us  [per_device(): lax.psum((jnp.stack([entry[0] for entry in local_pairs]), jnp.stack([entr...]
    psum x0 -> x5, blocking collectives: none -> 27.8 us  [per_device(): lax.psum(lax.psum((jnp.stack([entry[0] for entry in local_pairs]), jnp.st...]
    ppermute x18, waiting for transfers between devices: 28.5 us -> 9.56 us  [padded_2(): lax.ppermute(tail, axis, [(i, (i + 1) % count) for i in range(count)])]
    ppermute x18, waiting for transfers between devices: 6.81 us -> 15.7 us  [padded_2(): lax.ppermute(head, axis, [((i + 1) % count, i) for i in range(count)])]
    ppermute x18, starting transfers between devices: 26.5 us -> 18.5 us  [padded_2(): lax.ppermute(head, axis, [((i + 1) % count, i) for i in range(count)])]
    ppermute x18, starting transfers between devices: 5.81 us -> 13.1 us  [padded_2(): lax.ppermute(tail, axis, [(i, (i + 1) % count) for i in range(count)])]
  transfers between devices with their start and end apart: 36 -> 36, of which waited for: 16 -> 11; matrix products, arithmetic and copies ran while one was open for 12% -> 13% of each run, Pallas kernels for 0% -> 0%
where the time goes in v1:
time: 544 us; the launch traced here: 534 us
  blocking collectives  223 us (41%)
  other arithmetic  112 us (21%)
  between operations  88.9 us (16%)
  local copies, waits for them, and re-layouts  51.8 us (10%)
  starting transfers between devices  31.6 us (6%)
  waiting for transfers between devices  25.3 us (5%)
    psum x5, blocking collectives, per_device(): lax.psum((jnp.stack([entry[0] for entry in local_pairs]), jnp.stack([entr...  153 us
    reduce_sum x24, other arithmetic, block_apply(): real_part = jnp.sum(real_blocks * vec_real - imag_blocks * vec_imag, axis=1)  65.3 us
    psum x1, blocking collectives, per_device(): norm_sq = lax.psum(complex_dot(source, source)[0], ('ta', 'gz', 'xy'))  42.2 us
    psum x5, blocking collectives, per_device(): lax.psum(lax.psum((jnp.stack([entry[0] for entry in local_pairs]), jnp.st...  27.8 us
    scatter x30, local copies, waits for them, and re-layouts, per_device(): hessenberg.at[0, i, j].set(proj_reals[i]).at[1, i, j].set(proj_imags[i])  25.8 us
    ppermute x18, starting transfers between devices, padded_2(): lax.ppermute(head, axis, [((i + 1) % count, i) for i in range(count)])  18.5 us
    ppermute x18, waiting for transfers between devices, padded_2(): lax.ppermute(head, axis, [((i + 1) % count, i) for i in range(count)])  15.7 us
    sub x15, other arithmetic, scaled(): coef_real * vector[0] - coef_imag * vector[1]  13.2 us
  transfers between devices with their start and end apart: 36, of which 11 were waited for; matrix products, arithmetic and copies ran while one was open for 13% of the time, Pallas kernels for 0%

profile of v1, /device:TPU:0, one launch (start us, length us, event | category | flops | bytes accessed | tf_op | source)
XLA Modules:
  0.0 533.6 jit_solution(13808259968086942491)
XLA Ops:
  2.1 42.2 %psum.217 = f32[]{:T(128)} all-reduce(f32[]{:T(128)} %add_reduce_fusion.20), channel_id=1, replica_groups=mesh['ta'=2,'gz'=4,'xy'=4] {'ta','gz','xy'}, use_global_device_ids=true, to_apply=%region_1.0 | all-reduce | flops 1 | bytes 8 | tf_op jit(solution)/shard_map/psum | solution.py:106
  53.1 3.7 fusion.169
  59.2 3.0 fusion.25
  63.5 4.9 collective-permute-done.3
  68.4 3.8 fusion.97
  73.8 31.4 %all-reduce.6 = (f32[1]{0:T(128)}, f32[1]{0:T(128)}, f32[]{:T(128)}) all-reduce(f32[1]{0:T(128)} %bitcast.81, f32[1]{0:T(128)} %bitcast.83, f32[]{:T(128)} %get-tuple-element.653), channel_id=1, replica_groups=mesh['ta'=2,'gz'=4,'xy'=4] {'gz','xy'}, use_global_device_ids=true, to_apply=%region_21.22 | all-reduce | flops 3 | bytes 24 | tf_op jit(solution)/shard_map/psum | solution.py:115
  105.1 5.5 %all-reduce.11 = (f32[1]{0:T(128)}, f32[1]{0:T(128)}, f32[]{:T(128)}) all-reduce(f32[1]{0:T(128)} %get-tuple-element.666, f32[1]{0:T(128)} %get-tuple-element.667, f32[]{:T(128)} %get-tuple-element.668), channel_id=1, replica_groups=mesh['ta'=2,'gz'=4,'xy'=4] {'ta'}, use_global_device_ids=true, to_apply=%region_22.23 | all-reduce | flops 3 | bytes 24 | tf_op jit(solution)/shard_map/psum | solution.py:114
  122.6 3.7 fusion.173
  126.5 3.8 collective-permute-start.8
  134.6 3.7 fusion.101
  142.7 31.9 %all-reduce.5 = (f32[2]{0:T(128)S(1)}, f32[2]{0:T(128)S(1)}, f32[]{:T(128)}) all-reduce(f32[2]{0:T(128)S(1)} %pad_maximum_fusion.30, f32[2]{0:T(128)S(1)} %pad_maximum_fusion.31, f32[]{:T(128)} %get-tuple-element.650), channel_id=1, replica_groups=mesh['ta'=2,'gz'=4,'xy'=4] {'gz','xy'}, use_global_device_ids=true, to_apply=%region_49.50 | all-reduce | flops 5 | bytes 40 | tf_op jit(solution)/shard_map/psum | solution.py:115
  174.6 5.5 %all-reduce.10 = (f32[2]{0:T(128)S(1)}, f32[2]{0:T(128)S(1)}, f32[]{:T(128)}) all-reduce(f32[2]{0:T(128)S(1)} %get-tuple-element.663, f32[2]{0:T(128)S(1)} %get-tuple-element.664, f32[]{:T(128)} %get-tuple-element.665), channel_id=1, replica_groups=mesh['ta'=2,'gz'=4,'xy'=4] {'ta'}, use_global_device_ids=true, to_apply=%region_50.51 | all-reduce | flops 5 | bytes 40 | tf_op jit(solution)/shard_map/psum | solution.py:114
  193.9 3.7 fusion.177
  203.2 3.9 collective-permute-done.14
  207.2 3.7 fusion.105
  216.5 30.0 %all-reduce.4 = (f32[3]{0:T(128)S(1)}, f32[3]{0:T(128)S(1)}, f32[]{:T(128)}) all-reduce(f32[3]{0:T(128)S(1)} %pad_maximum_fusion.32, f32[3]{0:T(128)S(1)} %pad_maximum_fusion.33, f32[]{:T(128)} %get-tuple-element.647), channel_id=1, replica_groups=mesh['ta'=2,'gz'=4,'xy'=4] {'gz','xy'}, use_global_device_ids=true, to_apply=%region_80.81 | all-reduce | flops 7 | bytes 56 | tf_op jit(solution)/shard_map/psum | solution.py:115
  246.4 5.5 %all-reduce.9 = (f32[3]{0:T(128)S(1)}, f32[3]{0:T(128)S(1)}, f32[]{:T(128)}) all-reduce(f32[3]{0:T(128)S(1)} %get-tuple-element.660, f32[3]{0:T(128)S(1)} %get-tuple-element.661, f32[]{:T(128)} %get-tuple-element.662), channel_id=1, replica_groups=mesh['ta'=2,'gz'=4,'xy'=4] {'ta'}, use_global_device_ids=true, to_apply=%region_81.82 | all-reduce | flops 7 | bytes 56 | tf_op jit(solution)/shard_map/psum | solution.py:114
  270.5 3.7 fusion.181
  279.6 3.8 collective-permute-done.20
  283.4 3.7 fusion.109
  294.2 30.1 %all-reduce.3 = (f32[4]{0:T(128)S(1)}, f32[4]{0:T(128)S(1)}, f32[]{:T(128)}) all-reduce(f32[4]{0:T(128)S(1)} %pad_maximum_fusion.34, f32[4]{0:T(128)S(1)} %pad_maximum_fusion.35, f32[]{:T(128)} %get-tuple-element.642), channel_id=1, replica_groups=mesh['ta'=2,'gz'=4,'xy'=4] {'gz','xy'}, use_global_device_ids=true, to_apply=%region_113.114 | all-reduce | flops 9 | bytes 72 | tf_op jit(solution)/shard_map/psum | solution.py:115
  324.3 5.6 %all-reduce.8 = (f32[4]{0:T(128)S(1)}, f32[4]{0:T(128)S(1)}, f32[]{:T(128)}) all-reduce(f32[4]{0:T(128)S(1)} %get-tuple-element.657, f32[4]{0:T(128)S(1)} %get-tuple-element.658, f32[]{:T(128)} %get-tuple-element.659), channel_id=1, replica_groups=mesh['ta'=2,'gz'=4,'xy'=4] {'ta'}, use_global_device_ids=true, to_apply=%region_114.115 | all-reduce | flops 9 | bytes 72 | tf_op jit(solution)/shard_map/psum | solution.py:114
  349.5 3.7 fusion.185
  355.7 3.0 fusion.41
  358.6 3.7 collective-permute-done.26
  362.4 3.7 fusion.113
  368.4 3.2 stack.868
  371.6 3.3 stack.862
  374.9 30.0 %all-reduce.2 = (f32[5]{0:T(128)S(1)}, f32[5]{0:T(128)S(1)}, f32[]{:T(128)}) all-reduce(f32[5]{0:T(128)S(1)} %stack.862, f32[5]{0:T(128)S(1)} %stack.868, f32[]{:T(128)} %get-tuple-element.766), channel_id=1, replica_groups=mesh['ta'=2,'gz'=4,'xy'=4] {'gz','xy'}, use_global_device_ids=true, to_apply=%region_148.149 | all-reduce | flops 11 | bytes 88 | tf_op jit(solution)/shard_map/psum | solution.py:115
  404.8 5.5 %all-reduce.7 = (f32[5]{0:T(128)S(1)}, f32[5]{0:T(128)S(1)}, f32[]{:T(128)}) all-reduce(f32[5]{0:T(128)S(1)} %get-tuple-element.654, f32[5]{0:T(128)S(1)} %get-tuple-element.655, f32[]{:T(128)} %get-tuple-element.656), channel_id=1, replica_groups=mesh['ta'=2,'gz'=4,'xy'=4] {'ta'}, use_global_device_ids=true, to_apply=%region_149.150 | all-reduce | flops 11 | bytes 88 | tf_op jit(solution)/shard_map/psum | solution.py:114
  516.4 3.7 fusion.189
  528.1 3.7 fusion.117
  (295 shorter events, 144.8 us)
Async XLA Ops:
  45.7 11.1 %collective-permute-start = (f32[2,48,1,1,128]{4,3,2,1,0:T(1,128)S(1)}, f32[2,48,1,1,128]{4,3,2,1,0:T(1,128)S(1)}, u32[]{:S(2)}, u32[]{:S(2)}) collective-permute-start(f32[2,48,1,1,128]{4,3,2,1,0:T(1,128)S(1)} %broadcast_divide_fusion), channel_id=1, source_target_pairs={{16,0},{0,16},{17,1},{1,17},{18,2},{2,18},{19,3},{3,19},{20,4},{4,... | collective-permute-start | bytes 147464 | tf_op jit(solution)/shard_map/ppermute | solution.py:19
  48.1 8.7 %collective-permute-start.1 = (f32[2,48,1,1,128]{4,3,2,1,0:T(1,128)S(1)}, f32[2,48,1,1,128]{4,3,2,1,0:T(1,128)S(1)}, u32[]{:S(2)}, u32[]{:S(2)}) collective-permute-start(f32[2,48,1,1,128]{4,3,2,1,0:T(1,128)S(1)} %broadcast_divide_fusion), channel_id=1, source_target_pairs={{0,16},{16,0},{1,17},{17,1},{2,18},{18,2},{3,19},{19,3},{4,20},{20... | collective-permute-start | bytes 147464 | tf_op jit(solution)/shard_map/ppermute | solution.py:17
  48.3 3.9 collective-permute-start.4
  48.4 4.4 collective-permute-start.5
  57.0 6.5 %collective-permute-start.2 = (f32[2,48,3,1,128]{4,3,2,1,0:T(1,128)S(1)}, f32[2,48,3,1,128]{4,3,2,1,0:T(1,128)S(1)}, u32[]{:S(2)}, u32[]{:S(2)}) collective-permute-start(f32[2,48,3,1,128]{4,3,2,1,0:T(1,128)S(1)} %pad_maximum_fusion), channel_id=1, source_target_pairs={{4,0},{8,4},{12,8},{0,12},{5,1},{9,5},{13,9},{1,13},{6,2},{10,6},{... | collective-permute-start | bytes 442376 | tf_op jit(solution)/shard_map/ppermute | solution.py:19
  59.2 9.1 %collective-permute-start.3 = (f32[2,48,3,1,128]{4,3,2,1,0:T(1,128)S(1)}, f32[2,48,3,1,128]{4,3,2,1,0:T(1,128)S(1)}, u32[]{:S(2)}, u32[]{:S(2)}) collective-permute-start(f32[2,48,3,1,128]{4,3,2,1,0:T(1,128)S(1)} %pad_maximum_fusion), channel_id=1, source_target_pairs={{0,4},{4,8},{8,12},{12,0},{1,5},{5,9},{9,13},{13,1},{2,6},{6,10},{... | collective-permute-start | bytes 442376 | tf_op jit(solution)/shard_map/ppermute | solution.py:17
  116.2 10.1 %collective-permute-start.6 = (f32[2,48,1,1,128]{4,3,2,1,0:T(1,128)S(1)}, f32[2,48,1,1,128]{4,3,2,1,0:T(1,128)S(1)}, u32[]{:S(2)}, u32[]{:S(2)}) collective-permute-start(f32[2,48,1,1,128]{4,3,2,1,0:T(1,128)S(1)} %fusion.222), channel_id=1, source_target_pairs={{16,0},{0,16},{17,1},{1,17},{18,2},{2,18},{19,3},{3,19},{20,4},{4,... | collective-permute-start | bytes 147464 | tf_op jit(solution)/shard_map/ppermute | solution.py:19
  118.0 8.3 %collective-permute-start.7 = (f32[2,48,1,1,128]{4,3,2,1,0:T(1,128)S(1)}, f32[2,48,1,1,128]{4,3,2,1,0:T(1,128)S(1)}, u32[]{:S(2)}, u32[]{:S(2)}) collective-permute-start(f32[2,48,1,1,128]{4,3,2,1,0:T(1,128)S(1)} %fusion.222), channel_id=1, source_target_pairs={{0,16},{16,0},{1,17},{17,1},{2,18},{18,2},{3,19},{19,3},{4,20},{20... | collective-permute-start | bytes 147464 | tf_op jit(solution)/shard_map/ppermute | solution.py:17
  126.4 8.1 %collective-permute-start.9 = (f32[2,48,3,1,128]{4,3,2,1,0:T(1,128)S(1)}, f32[2,48,3,1,128]{4,3,2,1,0:T(1,128)S(1)}, u32[]{:S(2)}, u32[]{:S(2)}) collective-permute-start(f32[2,48,3,1,128]{4,3,2,1,0:T(1,128)S(1)} %pad_maximum_fusion.1), channel_id=1, source_target_pairs={{0,4},{4,8},{8,12},{12,0},{1,5},{5,9},{9,13},{13,1},{2,6},{6,10},{... | collective-permute-start | bytes 442376 | tf_op jit(solution)/shard_map/ppermute | solution.py:17
  126.5 8.1 %collective-permute-start.8 = (f32[2,48,3,1,128]{4,3,2,1,0:T(1,128)S(1)}, f32[2,48,3,1,128]{4,3,2,1,0:T(1,128)S(1)}, u32[]{:S(2)}, u32[]{:S(2)}) collective-permute-start(f32[2,48,3,1,128]{4,3,2,1,0:T(1,128)S(1)} %pad_maximum_fusion.1), channel_id=1, source_target_pairs={{4,0},{8,4},{12,8},{0,12},{5,1},{9,5},{13,9},{1,13},{6,2},{10,6},{... | collective-permute-start | bytes 442376 | tf_op jit(solution)/shard_map/ppermute | solution.py:19
  187.0 10.6 %collective-permute-start.12 = (f32[2,48,1,1,128]{4,3,2,1,0:T(1,128)S(1)}, f32[2,48,1,1,128]{4,3,2,1,0:T(1,128)S(1)}, u32[]{:S(2)}, u32[]{:S(2)}) collective-permute-start(f32[2,48,1,1,128]{4,3,2,1,0:T(1,128)S(1)} %fusion.262), channel_id=1, source_target_pairs={{16,0},{0,16},{17,1},{1,17},{18,2},{2,18},{19,3},{3,19},{20,4},{4,... | collective-permute-start | bytes 147464 | tf_op jit(solution)/shard_map/ppermute | solution.py:19
  188.8 8.7 %collective-permute-start.13 = (f32[2,48,1,1,128]{4,3,2,1,0:T(1,128)S(1)}, f32[2,48,1,1,128]{4,3,2,1,0:T(1,128)S(1)}, u32[]{:S(2)}, u32[]{:S(2)}) collective-permute-start(f32[2,48,1,1,128]{4,3,2,1,0:T(1,128)S(1)} %fusion.262), channel_id=1, source_target_pairs={{0,16},{16,0},{1,17},{17,1},{2,18},{18,2},{3,19},{19,3},{4,20},{20... | collective-permute-start | bytes 147464 | tf_op jit(solution)/shard_map/ppermute | solution.py:17
  189.4 4.1 collective-permute-start.16
  189.4 4.0 collective-permute-start.17
  197.7 9.4 %collective-permute-start.14 = (f32[2,48,3,1,128]{4,3,2,1,0:T(1,128)S(1)}, f32[2,48,3,1,128]{4,3,2,1,0:T(1,128)S(1)}, u32[]{:S(2)}, u32[]{:S(2)}) collective-permute-start(f32[2,48,3,1,128]{4,3,2,1,0:T(1,128)S(1)} %pad_maximum_fusion.2), channel_id=1, source_target_pairs={{4,0},{8,4},{12,8},{0,12},{5,1},{9,5},{13,9},{1,13},{6,2},{10,6},{... | collective-permute-start | bytes 442376 | tf_op jit(solution)/shard_map/ppermute | solution.py:19
  198.2 8.9 %collective-permute-start.15 = (f32[2,48,3,1,128]{4,3,2,1,0:T(1,128)S(1)}, f32[2,48,3,1,128]{4,3,2,1,0:T(1,128)S(1)}, u32[]{:S(2)}, u32[]{:S(2)}) collective-permute-start(f32[2,48,3,1,128]{4,3,2,1,0:T(1,128)S(1)} %pad_maximum_fusion.2), channel_id=1, source_target_pairs={{0,4},{4,8},{8,12},{12,0},{1,5},{5,9},{9,13},{13,1},{2,6},{6,10},{... | collective-permute-start | bytes 442376 | tf_op jit(solution)/shard_map/ppermute | solution.py:17
  260.2 13.9 %collective-permute-start.18 = (f32[2,48,1,1,128]{4,3,2,1,0:T(1,128)S(1)}, f32[2,48,1,1,128]{4,3,2,1,0:T(1,128)S(1)}, u32[]{:S(2)}, u32[]{:S(2)}) collective-permute-start(f32[2,48,1,1,128]{4,3,2,1,0:T(1,128)S(1)} %fusion.263), channel_id=1, source_target_pairs={{16,0},{0,16},{17,1},{1,17},{18,2},{2,18},{19,3},{3,19},{20,4},{4,... | collective-permute-start | bytes 147464 | tf_op jit(solution)/shard_map/ppermute | solution.py:19
  262.1 12.1 %collective-permute-start.19 = (f32[2,48,1,1,128]{4,3,2,1,0:T(1,128)S(1)}, f32[2,48,1,1,128]{4,3,2,1,0:T(1,128)S(1)}, u32[]{:S(2)}, u32[]{:S(2)}) collective-permute-start(f32[2,48,1,1,128]{4,3,2,1,0:T(1,128)S(1)} %fusion.263), channel_id=1, source_target_pairs={{0,16},{16,0},{1,17},{17,1},{2,18},{18,2},{3,19},{19,3},{4,20},{20... | collective-permute-start | bytes 147464 | tf_op jit(solution)/shard_map/ppermute | solution.py:17
  262.6 7.5 %collective-permute-start.22 = (f32[2,48,1,1,16]{4,3,2,1,0:T(1,128)S(1)}, f32[2,48,1,1,16]{4,3,2,1,0:T(1,128)S(1)}, u32[]{:S(2)}, u32[]{:S(2)}) collective-permute-start(f32[2,48,1,1,16]{4,3,2,1,0:T(1,128)S(1)} %get-tuple-element.812), channel_id=1, source_target_pairs={{1,0},{2,1},{3,2},{0,3},{5,4},{6,5},{7,6},{4,7},{9,8},{10,9},{11,1... | collective-permute-start | bytes 18440 | tf_op jit(solution)/shard_map/ppermute | solution.py:19
  262.7 7.4 %collective-permute-start.23 = (f32[2,48,1,1,16]{4,3,2,1,0:T(1,128)S(1)}, f32[2,48,1,1,16]{4,3,2,1,0:T(1,128)S(1)}, u32[]{:S(2)}, u32[]{:S(2)}) collective-permute-start(f32[2,48,1,1,16]{4,3,2,1,0:T(1,128)S(1)} %get-tuple-element.811), channel_id=1, source_target_pairs={{0,1},{1,2},{2,3},{3,0},{4,5},{5,6},{6,7},{7,4},{8,9},{9,10},{10,1... | collective-permute-start | bytes 18440 | tf_op jit(solution)/shard_map/ppermute | solution.py:17
  274.3 9.0 %collective-permute-start.20 = (f32[2,48,3,1,128]{4,3,2,1,0:T(1,128)S(1)}, f32[2,48,3,1,128]{4,3,2,1,0:T(1,128)S(1)}, u32[]{:S(2)}, u32[]{:S(2)}) collective-permute-start(f32[2,48,3,1,128]{4,3,2,1,0:T(1,128)S(1)} %pad_maximum_fusion.3), channel_id=1, source_target_pairs={{4,0},{8,4},{12,8},{0,12},{5,1},{9,5},{13,9},{1,13},{6,2},{10,6},{... | collective-permute-start | bytes 442376 | tf_op jit(solution)/shard_map/ppermute | solution.py:19
  274.4 8.9 %collective-permute-start.21 = (f32[2,48,3,1,128]{4,3,2,1,0:T(1,128)S(1)}, f32[2,48,3,1,128]{4,3,2,1,0:T(1,128)S(1)}, u32[]{:S(2)}, u32[]{:S(2)}) collective-permute-start(f32[2,48,3,1,128]{4,3,2,1,0:T(1,128)S(1)} %pad_maximum_fusion.3), channel_id=1, source_target_pairs={{0,4},{4,8},{8,12},{12,0},{1,5},{5,9},{9,13},{13,1},{2,6},{6,10},{... | collective-permute-start | bytes 442376 | tf_op jit(solution)/shard_map/ppermute | solution.py:17
  339.6 13.6 %collective-permute-start.24 = (f32[2,48,1,1,128]{4,3,2,1,0:T(1,128)S(1)}, f32[2,48,1,1,128]{4,3,2,1,0:T(1,128)S(1)}, u32[]{:S(2)}, u32[]{:S(2)}) collective-permute-start(f32[2,48,1,1,128]{4,3,2,1,0:T(1,128)S(1)} %fusion.246), channel_id=1, source_target_pairs={{16,0},{0,16},{17,1},{1,17},{18,2},{2,18},{19,3},{3,19},{20,4},{4,... | collective-permute-start | bytes 147464 | tf_op jit(solution)/shard_map/ppermute | solution.py:19
  341.4 11.8 %collective-permute-start.25 = (f32[2,48,1,1,128]{4,3,2,1,0:T(1,128)S(1)}, f32[2,48,1,1,128]{4,3,2,1,0:T(1,128)S(1)}, u32[]{:S(2)}, u32[]{:S(2)}) collective-permute-start(f32[2,48,1,1,128]{4,3,2,1,0:T(1,128)S(1)} %fusion.246), channel_id=1, source_target_pairs={{0,16},{16,0},{1,17},{17,1},{2,18},{18,2},{3,19},{19,3},{4,20},{20... | collective-permute-start | bytes 147464 | tf_op jit(solution)/shard_map/ppermute | solution.py:17
  342.0 7.2 %collective-permute-start.28 = (f32[2,48,1,1,16]{4,3,2,1,0:T(1,128)S(1)}, f32[2,48,1,1,16]{4,3,2,1,0:T(1,128)S(1)}, u32[]{:S(2)}, u32[]{:S(2)}) collective-permute-start(f32[2,48,1,1,16]{4,3,2,1,0:T(1,128)S(1)} %get-tuple-element.778), channel_id=1, source_target_pairs={{1,0},{2,1},{3,2},{0,3},{5,4},{6,5},{7,6},{4,7},{9,8},{10,9},{11,1... | collective-permute-start | bytes 18440 | tf_op jit(solution)/shard_map/ppermute | solution.py:19
  342.0 7.1 %collective-permute-start.29 = (f32[2,48,1,1,16]{4,3,2,1,0:T(1,128)S(1)}, f32[2,48,1,1,16]{4,3,2,1,0:T(1,128)S(1)}, u32[]{:S(2)}, u32[]{:S(2)}) collective-permute-start(f32[2,48,1,1,16]{4,3,2,1,0:T(1,128)S(1)} %get-tuple-element.777), channel_id=1, source_target_pairs={{0,1},{1,2},{2,3},{3,0},{4,5},{5,6},{6,7},{7,4},{8,9},{9,10},{10,1... | collective-permute-start | bytes 18440 | tf_op jit(solution)/shard_map/ppermute | solution.py:17
  353.4 9.0 %collective-permute-start.26 = (f32[2,48,3,1,128]{4,3,2,1,0:T(1,128)S(1)}, f32[2,48,3,1,128]{4,3,2,1,0:T(1,128)S(1)}, u32[]{:S(2)}, u32[]{:S(2)}) collective-permute-start(f32[2,48,3,1,128]{4,3,2,1,0:T(1,128)S(1)} %pad_maximum_fusion.4), channel_id=1, source_target_pairs={{4,0},{8,4},{12,8},{0,12},{5,1},{9,5},{13,9},{1,13},{6,2},{10,6},{... | collective-permute-start | bytes 442376 | tf_op jit(solution)/shard_map/ppermute | solution.py:19
  353.5 8.9 %collective-permute-start.27 = (f32[2,48,3,1,128]{4,3,2,1,0:T(1,128)S(1)}, f32[2,48,3,1,128]{4,3,2,1,0:T(1,128)S(1)}, u32[]{:S(2)}, u32[]{:S(2)}) collective-permute-start(f32[2,48,3,1,128]{4,3,2,1,0:T(1,128)S(1)} %pad_maximum_fusion.4), channel_id=1, source_target_pairs={{0,4},{4,8},{8,12},{12,0},{1,5},{5,9},{9,13},{13,1},{2,6},{6,10},{... | collective-permute-start | bytes 442376 | tf_op jit(solution)/shard_map/ppermute | solution.py:17
  509.8 10.3 %collective-permute-start.30 = (f32[2,48,1,1,128]{4,3,2,1,0:T(1,128)S(1)}, f32[2,48,1,1,128]{4,3,2,1,0:T(1,128)S(1)}, u32[]{:S(2)}, u32[]{:S(2)}) collective-permute-start(f32[2,48,1,1,128]{4,3,2,1,0:T(1,128)S(1)} %maximum_add_fusion.11), channel_id=1, source_target_pairs={{16,0},{0,16},{17,1},{1,17},{18,2},{2,18},{19,3},{3,19},{20,4},{4,... | collective-permute-start | bytes 147464 | tf_op jit(solution)/shard_map/ppermute | solution.py:19
  511.6 8.5 %collective-permute-start.31 = (f32[2,48,1,1,128]{4,3,2,1,0:T(1,128)S(1)}, f32[2,48,1,1,128]{4,3,2,1,0:T(1,128)S(1)}, u32[]{:S(2)}, u32[]{:S(2)}) collective-permute-start(f32[2,48,1,1,128]{4,3,2,1,0:T(1,128)S(1)} %maximum_add_fusion.11), channel_id=1, source_target_pairs={{0,16},{16,0},{1,17},{17,1},{2,18},{18,2},{3,19},{19,3},{4,20},{20... | collective-permute-start | bytes 147464 | tf_op jit(solution)/shard_map/ppermute | solution.py:17
  520.2 7.7 %collective-permute-start.32 = (f32[2,48,3,1,128]{4,3,2,1,0:T(1,128)S(1)}, f32[2,48,3,1,128]{4,3,2,1,0:T(1,128)S(1)}, u32[]{:S(2)}, u32[]{:S(2)}) collective-permute-start(f32[2,48,3,1,128]{4,3,2,1,0:T(1,128)S(1)} %pad_maximum_fusion.5), channel_id=1, source_target_pairs={{4,0},{8,4},{12,8},{0,12},{5,1},{9,5},{13,9},{1,13},{6,2},{10,6},{... | collective-permute-start | bytes 442376 | tf_op jit(solution)/shard_map/ppermute | solution.py:19
  520.3 7.7 %collective-permute-start.33 = (f32[2,48,3,1,128]{4,3,2,1,0:T(1,128)S(1)}, f32[2,48,3,1,128]{4,3,2,1,0:T(1,128)S(1)}, u32[]{:S(2)}, u32[]{:S(2)}) collective-permute-start(f32[2,48,3,1,128]{4,3,2,1,0:T(1,128)S(1)} %pad_maximum_fusion.5), channel_id=1, source_target_pairs={{0,4},{4,8},{8,12},{12,0},{1,5},{5,9},{9,13},{13,1},{2,6},{6,10},{... | collective-permute-start | bytes 442376 | tf_op jit(solution)/shard_map/ppermute | solution.py:17
  (8 other events, 78.8 us)
